TPU v7x, 32 devices: a whole 2x2x4 slice. The times are simulated.
32 devices in a mesh: leaf: 8 (over z, y), front: 4 (over x, core).
Axes of the slice: x: 2, y: 2, z: 4, core: 2. Of those that a mesh axis runs over, the one named last changes fastest.
Arguments:
- app_rhs: float32 [24576, 128], P(('leaf', 'front')), may hold values from -6 to 6
- pivot_source: int32 [24576], P(('leaf', 'front')), may hold values from 0 to 24575, as said below
- row_owner: int32 [24576], P(('leaf', 'front')), may hold values from 0 to 24575, as said below
- leaf_inverse: float32 [8, 4, 384, 1536], P('leaf', 'front'), may hold values from -1 to 2, as said below
- leaf_coupling: float32 [8, 4, 384, 1024], P('leaf', 'front'), may hold values from -0.07654656 to 0.07654656
- sep1_inverse: float32 [8, 4, 128, 1024], P('leaf', 'front'), may hold values from -1 to 2, as said below
- sep1_coupling: float32 [8, 4, 128, 2048], P('leaf', 'front'), may hold values from -0.09375 to 0.09375
- sep2_inverse: float32 [8, 4, 128, 2048], P('leaf', 'front'), may hold values from -1 to 2, as said below
- sep2_coupling: float32 [8, 4, 128, 4096], P('leaf', 'front'), may hold values from -0.06629126 to 0.06629126
- sep3_inverse: float32 [8, 4, 128, 4096], P('leaf', 'front'), may hold values from -1 to 2, as said below
Outputs:
- solution: float32 [24576, 128], P(('leaf', 'front'))
Inputs may be any that keep to these rules, and one draw needn't show every extreme that they name: `pivot_source`: A permutation. Row e of pivot_rhs comes from a device's block of 768 application rows; one block's rows go to at most 16 blocks of pivot rows, at most 60 rows from one block to one block, and some pair of blocks carries exactly 60 rows. The inverse of pivot_source: pivot_source[row_owner[i]] = i. `leaf_inverse`: each front's matrix is the identity plus dense entries of magnitude at most 2 / sqrt of the front's pivot rows. `sep1_inverse`: as leaf_inverse. `sep2_inverse`: as leaf_inverse. `sep3_inverse`: as leaf_inverse.
All inputs are finite; a program needn't handle non-finite values.
Results may differ from a plain program's by a relative error of at most 0.00011.
Values sent between devices are 32-bit elements; how exact they have to be, the bound alone decides.
A program may use at most 128 MiB of HBM per device.

v0:
```python
import functools

import jax
import jax.numpy as jnp
from jax import lax
from jax.experimental import pallas as pl
from jax.experimental.pallas import tpu as pltpu
from jax.sharding import PartitionSpec as P

LEAF_PIV = 384
SEP_PIV = 128
BLK = 128
CHUNK = 4
STRIPES = 8
MESH = pl.DeviceIdType.MESH


def ranked_slots(targets, bucket_count):
    one_hot = (targets[:, None] == jnp.arange(bucket_count, dtype=jnp.int32)[None, :]).astype(
        jnp.int32
    )
    running = jnp.cumsum(one_hot, axis=0) - one_hot
    return jnp.sum(running * one_hot, axis=1)


def move_rows(outgoing, slot_cap):
    leaves = lax.axis_size("leaf")
    fronts = lax.axis_size("front")
    rhs_count = outgoing.shape[1]
    shaped = outgoing.reshape(leaves * fronts, slot_cap, rhs_count)
    arrived = lax.all_to_all(shaped, ("leaf", "front"), split_axis=0, concat_axis=0, tiled=True)
    return arrived.reshape(leaves * fronts * slot_cap, rhs_count)


def bit_of(value, place):
    return lax.rem(lax.div(value, jnp.int32(2**place)), jnp.int32(2))


def stripe_orders(front_bits, height):
    front = [("front", place) for place in range(front_bits)]
    leaf = [("leaf", place) for place in range(height)]
    first = front + leaf
    second = front[:1] + leaf[:1] + front[1:] + leaf[1:]
    return (first, second)


def split(value):
    high = value.astype(jnp.bfloat16)
    return high, (value - high.astype(jnp.float32)).astype(jnp.bfloat16)


def product(left, right, right_axis):
    dims = (((1,), (right_axis,)), ((), ()))
    dot = functools.partial(lax.dot_general, dimension_numbers=dims, preferred_element_type=jnp.float32)
    left_high, left_low = left
    right_high, right_low = split(right)
    return dot(left_high, right_high) + (dot(left_low, right_high) + dot(left_high, right_low))


def solve_kernel(front_bits, stripe_rows, sizes, *refs):
    rhs_ref, *weights_hbm = refs[:8]
    out_ref = refs[8]
    weights = refs[9:16]
    buffers = refs[16:]
    stripes = len(stripe_rows)
    pos = 0

    def take(count):
        nonlocal pos
        pos += count
        return buffers[pos - count : pos]

    up = [take(stripes) for _ in range(4)]
    down = [None] + [take(stripes) for _ in range(3)]
    partial = take(stripes)
    up_recv = [None] + [take(stripes) for _ in range(3)]
    down_recv = [take(stripes) for _ in range(4)]
    solved = take(4)
    load_sems, send_sems, recv_sems = take(3)
    used = [0]

    leaf = lax.axis_index("leaf")
    front = lax.axis_index("front")
    here = {"leaf": leaf, "front": front}

    def partner(bit):
        axis, place = bit
        mine = bit_of(here[axis], place)
        other = here[axis] + (1 - 2 * mine) * 2**place
        return (other, front) if axis == "leaf" else (leaf, other)

    all_bits = [("front", place) for place in range(front_bits)] + [("leaf", place) for place in range(3)]
    barrier = pltpu.get_barrier_semaphore()
    for bit in all_bits:
        pl.semaphore_signal(barrier, inc=1, device_id=partner(bit), device_id_type=MESH)
    loads = []
    for index in range(7):
        load = pltpu.make_async_copy(weights_hbm[index], weights[index], load_sems.at[index])
        load.start()
        loads.append(load)
    pl.semaphore_wait(barrier, len(all_bits))

    def unit(height):
        return LEAF_PIV // BLK if height == 0 else 1

    def slot_of(block, height, stripe):
        piece = unit(height)
        static = isinstance(block, int)
        place, rest = divmod(block, piece) if static else (block, 0)
        order = stripe_orders(front_bits, height)[stripe % 2]
        slot = 0
        for axis, at in order:
            at = at + height if axis == "front" else at
            slot = slot * 2 + (place >> at & 1 if static else bit_of(place, at))
        return slot * piece + rest

    def remote(source, target, bit):
        index = used[0]
        used[0] += 1
        copy = pltpu.make_async_remote_copy(
            src_ref=source,
            dst_ref=target,
            send_sem=send_sems.at[index],
            recv_sem=recv_sems.at[index],
            device_id=partner(bit),
            device_id_type=MESH,
        )
        copy.start()
        return copy

    def own_slots(height):
        out = []
        for stripe in range(stripes):
            slot = 0
            for axis, at in stripe_orders(front_bits, height)[stripe % 2]:
                slot = slot * 2 + bit_of(here[axis], at)
            out.append(slot * unit(height))
        return out

    def reduce_group(height, bufs, recvs, middle):
        piece = unit(height)
        orders = stripe_orders(front_bits, height)
        depth = len(orders[0])
        bases = [jnp.int32(0)] * stripes
        half = 2**depth * piece
        offset = 0
        for step in range(depth + 1):
            copies = []
            whole, half = half, half // 2
            for stripe in range(stripes):
                if step > 0:
                    pending[stripe].wait()
                    keep = bases[stripe]

                    def add(index, carry, stripe=stripe, keep=keep, prior=prior):
                        bufs[stripe][keep + index] += recvs[stripe][prior + index]
                        return carry

                    lax.fori_loop(0, whole, add, 0)
                if step < depth:
                    bit = orders[stripe % 2][step]
                    mine = bit_of(here[bit[0]], bit[1])
                    away = bases[stripe] + (1 - mine) * half
                    bases[stripe] = bases[stripe] + mine * half
                    copies.append(
                        remote(bufs[stripe].at[pl.ds(away, half)], recvs[stripe].at[pl.ds(offset, half)], bit)
                    )
            if step == 0:
                middle()
            pending, prior = copies, offset
            offset += half

    def gather_group(height, bufs, middle):
        piece = unit(height)
        orders = stripe_orders(front_bits, height)
        depth = len(orders[0])
        bases = own_slots(height)
        size = piece
        pending = None
        for step in range(depth, -1, -1):
            copies = []
            if step == 0:
                middle()
            for stripe in range(stripes):
                if pending is not None:
                    pending[stripe].wait()
                if step > 0:
                    bit = orders[stripe % 2][step - 1]
                    span = pl.ds(bases[stripe], size)
                    copies.append(remote(bufs[stripe].at[span], bufs[stripe].at[span], bit))
                    bases[stripe] = bases[stripe] - bit_of(here[bit[0]], bit[1]) * size
            pending = copies
            size *= 2

    def splits(height):
        return unit(height) == 1 and 2**height % CHUNK == 0

    def chunks(height, side, body, carry):
        count = sizes[height] // BLK // CHUNK
        if unit(height) > 1:
            for index in range(count):
                slots = [
                    [slot_of(index * CHUNK + step, height, kind) for kind in range(2)] for step in range(CHUNK)
                ]
                carry = body(index * CHUNK * BLK, slots, carry)
            return carry

        def visit(index, carry):
            if side is not None:
                run = 2**height // CHUNK
                index = lax.div(index, jnp.int32(run)) * (2 * run) + side * run + lax.rem(index, jnp.int32(run))
            bases = [slot_of(index * CHUNK, height, kind) for kind in range(2)]
            slots = [[bases[kind] + slot_of(step, height, kind) for kind in range(2)] for step in range(CHUNK)]
            return body(pl.multiple_of(index * (CHUNK * BLK), CHUNK * BLK), slots, carry)

        return lax.fori_loop(0, count if side is None else count // 2, visit, carry)

    def apply_rows(weight, bufs, height, side, total):
        def body(start, slots, total):
            parts = [
                jnp.concatenate([bufs[s][slots[step][s % 2]] for s in range(stripes)], axis=0)
                for step in range(CHUNK)
            ]
            left = split(jnp.concatenate(parts, axis=1))
            return total + product(left, weight[:, pl.ds(start, CHUNK * BLK)], 1)

        return chunks(height, side, body, total)

    def apply_cols(weight, vector, bufs, height, side):
        left = split(vector)

        def body(start, slots, carry):
            result = product(left, weight[:, pl.ds(start, CHUNK * BLK)], 0)
            for step in range(CHUNK):
                low = 0
                for s in range(stripes):
                    bufs[s][slots[step][s % 2]] = result[low : low + stripe_rows[s], step * BLK : (step + 1) * BLK]
                    low += stripe_rows[s]
            return carry

        chunks(height, side, body, 0)

    core = bit_of(front, 0)

    def reduced(weight, vector, height, recvs):
        if splits(height):
            apply_cols(weight, vector, partial, height, 1 - core)
            reduce_group(
                height, partial, recvs, lambda: apply_cols(weight, vector, partial, height, core)
            )
        else:
            apply_cols(weight, vector, partial, height, None)
            reduce_group(height, partial, recvs, lambda: None)

    def gathered_rows(weight, bufs, height, ready):
        totals = [jnp.zeros((BLK, weight.shape[0]), jnp.float32)]

        def own_side():
            ready()
            if splits(height):
                totals.append(apply_rows(weight, bufs, height, core, totals[-1]))

        gather_group(height, bufs, own_side)
        return apply_rows(weight, bufs, height, 1 - core if splits(height) else None, totals[-1])

    def own_block(bufs, slots, part):
        return jnp.concatenate([bufs[s][slots[s] + part] for s in range(stripes)], axis=0)

    def set_block(bufs, slots, part, value):
        low = 0
        for s in range(stripes):
            bufs[s][slots[s] + part] = value[low : low + stripe_rows[s]]
            low += stripe_rows[s]

    inverses = (weights[0], weights[2], weights[4], weights[6])
    couplings = (weights[1], weights[3], weights[5])
    starts = (0, LEAF_PIV, LEAF_PIV + SEP_PIV, LEAF_PIV + 2 * SEP_PIV)
    for height in range(4):
        slots = own_slots(height)
        if height > 0:
            loads[2 * height - 1].wait()
            reduced(couplings[height - 1], solved[height - 1][...], height, up_recv[height])
        for part in range(unit(height)):
            low = starts[height] + part * BLK
            value = rhs_ref[low : low + BLK, :].T
            if height > 0:
                value = value - own_block(partial, slots, part)
            set_block(up[height], slots, part, value)
        solved[height][...] = gathered_rows(inverses[height], up[height], height, loads[2 * height].wait)
    for height in (3, 2, 1, 0):
        target = solved[height][...]
        if height < 3:
            target = target - gathered_rows(couplings[height], down[height + 1], height + 1, lambda: None)
        reduced(inverses[height], target, height, down_recv[height])
        slots = own_slots(height)
        for part in range(unit(height)):
            low = starts[height] + part * BLK
            value = own_block(partial, slots, part)
            out_ref[low : low + BLK, :] = value.T
            if height > 0:
                set_block(down[height], slots, part, value)


def solve(ordered, weights):
    leaves = lax.axis_size("leaf")
    fronts = lax.axis_size("front")
    front_bits = fronts.bit_length() - 1
    rhs_count = ordered.shape[1]
    stripe_rows = (rhs_count // STRIPES,) * STRIPES
    sizes = tuple(w.shape[1] for w in (weights[0], weights[2], weights[4], weights[6]))
    scratch = [pltpu.VMEM(w.shape, jnp.float32) for w in weights]

    def stripe_buffers(blocks):
        return [pltpu.VMEM((blocks, rows, BLK), jnp.float32) for rows in stripe_rows]

    counts = [size // BLK for size in sizes]
    copies = 0
    for height in range(4):
        copies += (2 if height == 0 else 4) * (front_bits + height) * len(stripe_rows)
    for blocks in counts + counts[1:] + [max(counts)] + counts[1:] + counts:
        scratch += stripe_buffers(blocks)
    scratch += [pltpu.VMEM((rhs_count, rows), jnp.float32) for rows in (LEAF_PIV, SEP_PIV, SEP_PIV, SEP_PIV)]
    scratch += [
        pltpu.SemaphoreType.DMA((7,)),
        pltpu.SemaphoreType.DMA((copies,)),
        pltpu.SemaphoreType.DMA((copies,)),
    ]
    vmem = pl.BlockSpec(memory_space=pltpu.VMEM)
    return pl.pallas_call(
        functools.partial(solve_kernel, front_bits, stripe_rows, sizes),
        out_shape=jax.ShapeDtypeStruct(ordered.shape, jnp.float32),
        in_specs=[vmem] + [pl.BlockSpec(memory_space=pl.ANY)] * 7,
        out_specs=vmem,
        scratch_shapes=scratch,
        compiler_params=pltpu.CompilerParams(
            collective_id=0, has_side_effects=True, vmem_limit_bytes=66 * 1024 * 1000
        ),
    )(ordered, *weights)


def per_device(
    app_rhs,
    pivot_source,
    row_owner,
    leaf_inverse,
    leaf_coupling,
    sep1_inverse,
    sep1_coupling,
    sep2_inverse,
    sep2_coupling,
    sep3_inverse,
):
    row_count = app_rhs.shape[0]
    rhs_count = app_rhs.shape[1]
    peer_count = lax.axis_size("leaf") * lax.axis_size("front")
    mean_rows = row_count // (peer_count // 2)
    slot_cap = mean_rows + max(1, mean_rows // 4)
    destination = row_owner // row_count
    send_index = destination * slot_cap + ranked_slots(destination, peer_count)
    anchor = pivot_source // row_count
    same_source = (anchor[:, None] == anchor[None, :]) & (
        pivot_source[None, :] < pivot_source[:, None]
    )
    recv_index = anchor * slot_cap + jnp.sum(same_source.astype(jnp.int32), axis=1)
    outgoing = (
        jnp.zeros((peer_count * slot_cap, rhs_count), jnp.float32).at[send_index].set(app_rhs)
    )
    ordered = move_rows(outgoing, slot_cap)[recv_index]
    weights = [
        w[0, 0]
        for w in (
            leaf_inverse,
            leaf_coupling,
            sep1_inverse,
            sep1_coupling,
            sep2_inverse,
            sep2_coupling,
            sep3_inverse,
        )
    ]
    pivot_order = solve(ordered, weights)
    returning = (
        jnp.zeros((peer_count * slot_cap, rhs_count), jnp.float32).at[recv_index].set(pivot_order)
    )
    returned = move_rows(returning, slot_cap)
    return returned[send_index]


def solution(mesh):
    in_specs = (
        P(("leaf", "front"), None),
        P(("leaf", "front")),
        P(("leaf", "front")),
        P("leaf", "front", None, None),
        P("leaf", "front", None, None),
        P("leaf", "front", None, None),
        P("leaf", "front", None, None),
        P("leaf", "front", None, None),
        P("leaf", "front", None, None),
        P("leaf", "front", None, None),
    )
    out_specs = P(("leaf", "front"), None)
    return jax.shard_map(
        per_device, mesh=mesh, in_specs=in_specs, out_specs=out_specs, check_vma=False
    )
```

profile of v0, /device:TPU:0, one launch (start us, length us, event | category | flops | bytes accessed | tf_op | source)
XLA Modules:
  0.0 262.2 jit_solution(1258930866032873491)
XLA Ops:
  0.0 0.7 add_select_fusion
  0.7 1.7 reduce-window.6
  2.5 0.3 slice_reduce_fusion
  2.7 0.1 fusion.6
  2.9 0.7 compare_select_fusion
  3.6 0.0 copy-start.1
  3.6 0.0 copy-start
  3.6 4.8 %scatter_custom_fusion = f32[1920,128]{1,0:T(8,128)S(1)} fusion(s32[768]{0:T(1024)S(1)} %compare_select_fusion, f32[768,128]{1,0:T(8,128)} %param.10, f32[]{:T(128)} %constant.19.clone.1), kind=kCustom, calls=%fused_computation.7 | custom fusion | bytes 983552 | tf_op jit(solution)/shard_map/scatter | solution.py:366
  8.4 1.1 reshape.33
  9.5 0.0 copy-done.1
  9.5 7.5 %all-to-all-start = ((f32[32,60,128]{2,1,0:T(8,128)}), f32[32,60,128]{2,1,0:T(8,128)S(1)}, u32[]{:S(2)}, u32[]{:S(2)}) async-start(f32[32,60,128]{2,1,0:T(8,128)} %reshape.33), calls=%async_computation | async-start | bytes 2097152 | tf_op jit(solution)/shard_map/all_to_all | solution.py:31
  17.0 0.0 copy-done
  17.0 0.5 convert_reduce_fusion
  17.6 0.0 copy-start.3
  17.6 0.6 copy-done.3
  18.2 24.8 %all-to-all-done = f32[32,60,128]{2,1,0:T(8,128)S(1)} async-done(((f32[32,60,128]{2,1,0:T(8,128)}), f32[32,60,128]{2,1,0:T(8,128)S(1)}, u32[]{:S(2)}, u32[]{:S(2)}) %all-to-all-start) | async-done | bytes 983072 | tf_op jit(solution)/shard_map/all_to_all | solution.py:31
  43.0 0.1 reshape.34
  43.1 2.3 gather_fusion
  45.4 178.6 %shard_map.100 = f32[768,128]{1,0:T(8,128)} custom-call(f32[768,128]{1,0:T(8,128)} %gather_fusion, f32[384,1536]{1,0:T(8,128)} %bitcast.29, f32[384,1024]{1,0:T(8,128)} %bitcast.32, f32[128,1024]{1,0:T(8,128)} %bitcast.35, f32[128,2048]{1,0:T(8,128)} %bitcast.33, f32[128,2048]{1,0:T(8,128)} %bitcast.34, f32[128,4096]{1,0:T(8,128)} %bitcast.30, ...), custom_call_target="tpu_custom_call" | custom-call | tf_op jit(solution)/shard_map/pallas_call | solution.py:329
  223.9 0.0 copy-start.2
  223.9 5.0 %scatter_custom_fusion.1 = f32[1920,128]{1,0:T(8,128)S(1)} fusion(s32[768]{0:T(1024)} %copy-done.3, f32[768,128]{1,0:T(8,128)} %shard_map.100, f32[]{:T(128)} %constant.19.clone.1), kind=kCustom, calls=%fused_computation.5 | custom fusion | bytes 983552 | tf_op jit(solution)/shard_map/scatter | solution.py:383
  229.0 1.1 reshape.35
  230.0 3.6 %all-to-all-start.1 = ((f32[32,60,128]{2,1,0:T(8,128)}), f32[32,60,128]{2,1,0:T(8,128)S(1)}, u32[]{:S(2)}, u32[]{:S(2)}) async-start(f32[32,60,128]{2,1,0:T(8,128)} %reshape.35), calls=%async_computation.1 | async-start | bytes 2097152 | tf_op jit(solution)/shard_map/all_to_all | solution.py:31
  233.7 0.0 copy-done.2
  233.7 26.2 %all-to-all-done.1 = f32[32,60,128]{2,1,0:T(8,128)S(1)} async-done(((f32[32,60,128]{2,1,0:T(8,128)}), f32[32,60,128]{2,1,0:T(8,128)S(1)}, u32[]{:S(2)}, u32[]{:S(2)}) %all-to-all-start.1) | async-done | bytes 983072 | tf_op jit(solution)/shard_map/all_to_all | solution.py:31
  259.9 0.1 reshape.36
  259.9 2.3 gather_fusion.1
  (6 shorter events, 0.1 us)
Async XLA Ops:
  3.6 5.9 %copy-start.1 = (s32[768]{0:T(1024)}, s32[768]{0:T(1024)S(1)}, u32[]{:S(2)}) copy-start(s32[768]{0:T(1024)S(1)} %compare_select_fusion) | copy-start | bytes 9220
  3.6 13.4 %copy-start = (s32[768]{0:T(1024)S(1)}, s32[768]{0:T(1024)}, u32[]{:S(2)}) copy-start(s32[768]{0:T(1024)} %param.11) | copy-start | bytes 9220
  9.5 33.5 %all-to-all-start = ((f32[32,60,128]{2,1,0:T(8,128)}), f32[32,60,128]{2,1,0:T(8,128)S(1)}, u32[]{:S(2)}, u32[]{:S(2)}) async-start(f32[32,60,128]{2,1,0:T(8,128)} %reshape.33), calls=%async_computation | async-start | bytes 2097152 | tf_op jit(solution)/shard_map/all_to_all | solution.py:31
  17.6 0.6 copy-start.3
  223.9 9.7 %copy-start.2 = (s32[768]{0:T(1024)S(1)}, s32[768]{0:T(1024)}, u32[]{:S(2)}) copy-start(s32[768]{0:T(1024)} %copy-done.1) | copy-start | bytes 9220
  230.0 29.8 %all-to-all-start.1 = ((f32[32,60,128]{2,1,0:T(8,128)}), f32[32,60,128]{2,1,0:T(8,128)S(1)}, u32[]{:S(2)}, u32[]{:S(2)}) async-start(f32[32,60,128]{2,1,0:T(8,128)} %reshape.35), calls=%async_computation.1 | async-start | bytes 2097152 | tf_op jit(solution)/shard_map/all_to_all | solution.py:31
where the time goes:
time: 263 us; the launch traced here: 262 us
  Pallas kernels  179 us (68%)
  waiting for transfers between devices  51 us (19%)
  local copies, waits for them, and re-layouts  17.5 us (7%)
  starting transfers between devices  11.1 us (4%)
  other arithmetic  3.87 us (1%)
    pallas_call x1, Pallas kernels, solve(): pl.pallas_call(functools.partial(solve_kernel, front_bits, stripe_rows, s...  179 us
    all_to_all x2, waiting for transfers between devices, move_rows(): lax.all_to_all(shaped, ('leaf', 'front'), split_axis=0, concat_axis=0, ti...  51 us
    all_to_all x2, starting transfers between devices, move_rows(): lax.all_to_all(shaped, ('leaf', 'front'), split_axis=0, concat_axis=0, ti...  11.1 us
  transfers between devices with their start and end apart: 2, of which 2 were waited for; matrix products, arithmetic and copies ran while one was open for 0% of the time, Pallas kernels for 0%

commit v1 on v0

v1 whole, which is shorter than its diff:
```python
import functools

import jax
import jax.numpy as jnp
from jax import lax
from jax.experimental import pallas as pl
from jax.experimental.pallas import tpu as pltpu
from jax.sharding import PartitionSpec as P

BLK = 128
HEIGHTS = 4
CLASSES = 3
MESH = pl.DeviceIdType.MESH
CORE = ("front", 0)
STRIPE_UNITS = (3, 3, 3, 2, 2, 3)


def bit_of(value, place):
    return lax.rem(lax.div(value, jnp.int32(2**place)), jnp.int32(2))


def flipped(value, mask, bits):
    out = jnp.int32(0)
    for place in range(bits):
        out = out + lax.rem(bit_of(value, place) + bit_of(mask, place), jnp.int32(2)) * 2**place
    return out


def group_dims(front_bits, height):
    return [("front", place) for place in range(1, front_bits)] + [("leaf", place) for place in range(height)]


def group_orders(front_bits, height):
    dims = group_dims(front_bits, height)
    turns = min(CLASSES, len(dims))
    head, rest = dims[:turns], dims[turns:]
    return [head[turn:] + head[:turn] + rest for turn in range(turns)]


def place_slot(place, height, order):
    slot = 0
    for axis, at in order:
        slot = slot * 2 + (place >> (at + height if axis == "front" else at) & 1)
    return slot


def place_lane(place):
    return bin(place).count("1") % 2


def split(value):
    high = value.astype(jnp.bfloat16)
    return high, (value - high.astype(jnp.float32)).astype(jnp.bfloat16)


def dot(left, right, right_axis):
    dims = (((1,), (right_axis,)), ((), ()))
    return lax.dot_general(left, right, dimension_numbers=dims, preferred_element_type=jnp.float32)


def solve_kernel(leaf_bits, front_bits, stripe_rows, pivots, sizes, cap, *refs):
    app_ref, pack_idx, order_idx, back_pack_idx, back_idx = refs[:5]
    weights_hbm = refs[5:12]
    out_ref = refs[12]
    packed, arrived, returned, ordered, sol = refs[13:18]
    stages = refs[18]
    stacked = refs[19:26]
    left_ref = refs[26]
    solved = refs[27:31]
    buffers = refs[31:-7]
    load_sems, send_sems, recv_sems, go_send, go_recv, back_send, back_recv = refs[-7:]
    stripes = len(stripe_rows)
    lows = [sum(stripe_rows[:s]) for s in range(stripes)]
    pos = 0

    def take(count):
        nonlocal pos
        pos += count
        return buffers[pos - count : pos]

    partial = [take(stripes) for _ in range(HEIGHTS)]
    recv = [take(stripes) for _ in range(HEIGHTS)]
    whole_vec = [partial[0]] + [take(stripes) for _ in range(HEIGHTS - 1)]
    used = [0]

    leaf = lax.axis_index("leaf")
    front = lax.axis_index("front")
    fronts = 2**front_bits
    peers = 2 ** (front_bits + leaf_bits)
    here = {"leaf": leaf, "front": front}
    me = leaf * fronts + front

    def mine(dim):
        return bit_of(here[dim[0]], dim[1])

    core_flip = front + (1 - 2 * mine(CORE))

    def partner(dim):
        axis, place = dim
        if dim == CORE:
            return (leaf, core_flip)
        move = (1 - 2 * mine(dim)) * 2**place
        return (leaf + move, core_flip) if axis == "leaf" else (leaf, core_flip + move)

    def peer(step):
        turn = jnp.int32(peers - 1) - step
        return (
            flipped(leaf, lax.div(turn, jnp.int32(fronts)), leaf_bits),
            flipped(front, lax.rem(turn, jnp.int32(fronts)), front_bits),
        )

    piece_of = [pivots[h] // BLK for h in range(HEIGHTS)]
    halves = [size // BLK // 2 for size in sizes]
    orders = [group_orders(front_bits, h) for h in range(HEIGHTS)]
    lanes = []
    for height in range(HEIGHTS):
        total = jnp.int32(0)
        for place in range(front_bits):
            total = total + bit_of(front, place)
        for place in range(height):
            total = total + bit_of(leaf, place)
        lanes.append(lax.rem(total, jnp.int32(2)))

    def kind(height, stripe):
        return stripe % len(orders[height])

    perms = []
    for height in range(HEIGHTS):
        table = [[0] * halves[height] for _ in orders[height]]
        for place in range(2 ** (front_bits + height)):
            canon = place_slot(place, height, orders[height][0])
            for k, order in enumerate(orders[height]):
                for part in range(piece_of[height]):
                    table[k][canon * piece_of[height] + part] = (
                        place_slot(place, height, order) * piece_of[height] + part
                    )
        perms.append(table)

    weight_heights = (0, 1, 1, 2, 2, 3, 3)
    pieces = []
    for index in range(7):
        for part in range(weights_hbm[index].shape[0] // BLK):
            pieces.append((index, part))

    def stage_copy(number):
        index, part = pieces[number]
        return pltpu.make_async_copy(
            weights_hbm[index].at[pl.ds(part * BLK, BLK)],
            stages.at[number % 2, :, pl.ds(0, weights_hbm[index].shape[1])],
            load_sems.at[number % 2],
        )

    stage_copy(0).start()
    stage_copy(1).start()

    barrier = pltpu.get_barrier_semaphore()

    def greet(step, carry):
        pl.semaphore_signal(barrier, inc=1, device_id=peer(step), device_id_type=MESH)
        return carry

    lax.fori_loop(0, peers - 1, greet, 0)

    def pack_rows(index, source, target, base, where):
        for row in range(cap):
            target[base + row] = source(index[where + row])

    def send_to(step, source, target, sends, recvs):
        to_leaf, to_front = peer(step)
        there = to_leaf * fronts + to_front
        return pltpu.make_async_remote_copy(
            src_ref=source.at[pl.ds(there * cap, cap)],
            dst_ref=target.at[pl.ds(me * cap, cap)],
            send_sem=sends.at[step],
            recv_sem=recvs.at[step],
            device_id=(to_leaf, to_front),
            device_id_type=MESH,
        )

    def exchange_rows(index, source, target, sends, recvs, ready):
        def pack(step):
            to_leaf, to_front = peer(step)
            base = (to_leaf * fronts + to_front) * cap
            pack_rows(index, source, packed, base, base)

        pack(jnp.int32(0))
        ready()

        def body(step, carry):
            pack(step)
            send_to(step - 1, packed, target, sends, recvs).start()
            return carry

        lax.fori_loop(1, peers - 1, body, 0)
        pack_rows(index, source, target, me * cap, me * cap)
        send_to(jnp.int32(peers - 2), packed, target, sends, recvs).start()

    def finish_rows(target, sends, recvs):
        def body(step, carry):
            send_to(step, packed, target, sends, recvs).wait()
            return carry

        lax.fori_loop(0, peers - 1, body, 0)

    def unpack_rows(index, source, target):
        def body(group, carry):
            for row in range(8):
                target[group, pl.ds(row, 1), :] = source[index[group * 8 + row]]
            return carry

        lax.fori_loop(0, target.shape[0], body, 0, unroll=2)

    exchange_rows(
        pack_idx,
        lambda i: app_ref[i],
        arrived,
        go_send,
        go_recv,
        lambda: pl.semaphore_wait(barrier, peers - 1),
    )

    for number, (index, part) in enumerate(pieces):
        height = weight_heights[index]
        piece = piece_of[height]
        rows, cols = weights_hbm[index].shape
        stage_copy(number).wait()

        def convert(group, carry, number=number, index=index, part=part, height=height, rows=rows, cols=cols, piece=piece):
            span = pl.ds(pl.multiple_of(group * 16, 16), 16)
            high_rows = pl.ds(pl.multiple_of(part * BLK + group * 16, 16), 16)
            low_rows = pl.ds(pl.multiple_of(rows + part * BLK + group * 16, 16), 16)
            for block in range(cols // BLK):
                place, rest = divmod(block, piece)
                lane = place_lane(place)
                at = place_slot(place, height, orders[height][0]) * piece + rest
                high, low = split(stages[number % 2, span, pl.ds(block * BLK, BLK)])
                stacked[index][lane, high_rows, pl.ds(at * BLK, BLK)] = high
                stacked[index][lane, low_rows, pl.ds(at * BLK, BLK)] = low
            return carry

        lax.fori_loop(0, BLK // 16, convert, 0)
        if number + 2 < len(pieces):
            stage_copy(number + 2).start()

    finish_rows(arrived, go_send, go_recv)
    unpack_rows(order_idx, arrived, ordered)

    def remote(source, target, dim):
        index = used[0]
        used[0] += 1
        copy = pltpu.make_async_remote_copy(
            src_ref=source,
            dst_ref=target,
            send_sem=send_sems.at[index],
            recv_sem=recv_sems.at[index],
            device_id=partner(dim),
            device_id_type=MESH,
        )
        copy.start()
        return copy

    def own_slots(height):
        out = []
        for stripe in range(stripes):
            slot = jnp.int32(0)
            for dim in orders[height][kind(height, stripe)]:
                slot = slot * 2 + mine(dim)
            out.append(lanes[height] * halves[height] + slot * piece_of[height])
        return out

    def own_block(bufs, slots, part):
        return jnp.concatenate([bufs[s][slots[s] + part] for s in range(stripes)], axis=0)

    def reduce_steps(height, swap_at, fill):
        bufs, recvs, result = partial[height], recv[height], whole_vec[height]
        swap = swap_at is not None
        half = halves[height]
        lane = lanes[height]
        fill(1 - lane)
        pending = [
            remote(bufs[s].at[pl.ds((1 - lane) * half, half)], recvs[s].at[pl.ds(0, half)], CORE)
            for s in range(stripes)
        ]
        fill(lane)
        bases = [lane * half] * stripes
        depth = len(orders[height][0])
        whole, prior, offset = half, 0, half
        for step in range(depth + 1):
            full = swap and step == depth - 1
            size = whole if full else whole // 2
            if full:
                offset = swap_at
            copies = []
            for s in range(stripes):
                pending[s].wait()
                keep = pl.ds(bases[s], whole)
                (result if step == depth else bufs)[s][keep] = bufs[s][keep] + recvs[s][pl.ds(prior, whole)]
                if step < depth:
                    dim = orders[height][kind(height, s)][step]
                    away = bases[s]
                    if not full:
                        away = bases[s] + (1 - mine(dim)) * size
                        bases[s] = bases[s] + mine(dim) * size
                    copies.append(remote(bufs[s].at[pl.ds(away, size)], recvs[s].at[pl.ds(offset, size)], dim))
            pending, prior, whole = copies, offset, size
            offset += size
        return bases

    def gather_steps(height, bufs, bases, size, depth, middle):
        half = halves[height]
        pending = None
        for step in range(depth - 1, -2, -1):
            copies = []
            for s in range(stripes):
                if pending is not None:
                    pending[s].wait()
                dim = CORE if step < 0 else orders[height][kind(height, s)][step]
                span = pl.ds(bases[s], size)
                copies.append(remote(bufs[s].at[span], bufs[s].at[span], dim))
                if step >= 0:
                    bases[s] = bases[s] - mine(dim) * size
            pending = copies
            size *= 2
        middle()
        for copy in pending:
            copy.wait()

    def apply_rows(index, height, bufs, lane):
        half = halves[height]
        for at in range(half):
            block = jnp.concatenate(
                [bufs[s][lane * half + perms[height][kind(height, s)][at]] for s in range(stripes)], axis=0
            )
            high, low = split(block)
            left_ref[0:BLK, at * BLK : (at + 1) * BLK] = high
            left_ref[BLK : 2 * BLK, at * BLK : (at + 1) * BLK] = low
        full = dot(left_ref[:, 0 : half * BLK], stacked[index][lane], 1)
        both = full[:BLK] + full[BLK:]
        rows = both.shape[1] // 2
        return both[:, :rows] + both[:, rows:]

    def apply_cols(index, height, bufs, vector, lane):
        half = halves[height]
        high, low = split(vector)
        left = jnp.concatenate(
            [jnp.concatenate([high, high], axis=1), jnp.concatenate([low, low], axis=1)], axis=0
        )
        for at in range(0, half, 2):
            full = dot(left, stacked[index][lane, :, at * BLK : (at + 2) * BLK], 0)
            both = full[:BLK] + full[BLK:]
            for step in range(2):
                for s in range(stripes):
                    bufs[s][lane * half + perms[height][kind(height, s)][at + step]] = both[
                        lows[s] : lows[s] + stripe_rows[s], step * BLK : (step + 1) * BLK
                    ]

    def gathered_rows(index, height, bufs, bases, size, depth):
        lane = lanes[height]
        parts = []
        gather_steps(
            height, bufs, bases, size, depth, lambda: parts.append(apply_rows(index, height, bufs, lane))
        )
        return parts[0] + apply_rows(index, height, bufs, 1 - lane)

    inverses = (0, 2, 4, 6)
    couplings = (1, 3, 5)
    starts = [sum(pivots[:h]) for h in range(HEIGHTS)]

    def right_side(height, part):
        low = (starts[height] + part * BLK) // 8
        return ordered[low : low + BLK // 8].reshape(BLK, -1).T

    def keep_solution(height, slots):
        for part in range(piece_of[height]):
            low = starts[height] + part * BLK
            sol[low : low + BLK, :] = own_block(whole_vec[height], slots, part).T

    slots = own_slots(0)
    for part in range(piece_of[0]):
        value = right_side(0, part)
        for s in range(stripes):
            partial[0][s][slots[s] + part] = value[lows[s] : lows[s] + stripe_rows[s]]
    solved[0][...] = gathered_rows(
        inverses[0], 0, partial[0], slots, piece_of[0], len(orders[0][0])
    )
    for height in range(1, HEIGHTS):
        vector = -solved[height - 1][...]
        bufs = partial[height]

        def fill(lane, height=height, vector=vector, bufs=bufs):
            apply_cols(couplings[height - 1], height, bufs, vector, lane)
            if lane is lanes[height]:
                value = right_side(height, 0)
                slots = own_slots(height)
                for s in range(stripes):
                    bufs[s][slots[s]] = bufs[s][slots[s]] + value[lows[s] : lows[s] + stripe_rows[s]]

        bases = reduce_steps(height, 2 * halves[height] - 2, fill)
        solved[height][...] = gathered_rows(
            inverses[height], height, whole_vec[height], bases, 2, len(orders[height][0]) - 1
        )
    target = solved[HEIGHTS - 1][...]
    for height in range(HEIGHTS - 1, -1, -1):
        bufs = partial[height]

        def fill(lane, height=height, vector=target, bufs=bufs):
            apply_cols(inverses[height], height, bufs, vector, lane)

        bases = reduce_steps(height, 2 * halves[height] if height > 0 else None, fill)
        keep_solution(height, own_slots(height))
        if height > 0:
            target = solved[height - 1][...] - gathered_rows(
                couplings[height - 1], height, whole_vec[height], bases, 2, len(orders[height][0]) - 1
            )

    exchange_rows(
        back_pack_idx, lambda i: sol[pl.ds(i, 1), :], returned, back_send, back_recv, lambda: None
    )
    finish_rows(returned, back_send, back_recv)
    unpack_rows(back_idx, returned, out_ref)


def solve(app_rhs, tables, weights, cap):
    leaves = lax.axis_size("leaf")
    fronts = lax.axis_size("front")
    peers = leaves * fronts
    front_bits = fronts.bit_length() - 1
    leaf_bits = leaves.bit_length() - 1
    rows, rhs_count = app_rhs.shape
    units = [unit * rhs_count // BLK for unit in STRIPE_UNITS]
    stripe_rows = tuple(8 * unit for unit in units)
    inverses = (weights[0], weights[2], weights[4], weights[6])
    sizes = tuple(w.shape[1] for w in inverses)
    pivots = tuple(w.shape[0] for w in inverses)
    blocks = [size // BLK for size in sizes]

    def stripe_buffers(count):
        return [pltpu.VMEM((count, height, BLK), jnp.float32) for height in stripe_rows]

    copies = 0
    for height in range(HEIGHTS):
        depth = len(group_dims(front_bits, height))
        copies += 2 * (depth + 1) if height == 0 else 2 * (2 * depth + 1)
    copies *= len(stripe_rows)
    scratch = [
        pltpu.VMEM((peers * cap, 1, rhs_count), jnp.float32),
        pltpu.VMEM((peers * cap, 1, rhs_count), jnp.float32),
        pltpu.VMEM((peers * cap, 1, rhs_count), jnp.float32),
        pltpu.VMEM((rows // 8, 8, rhs_count), jnp.float32),
        pltpu.VMEM((rows, rhs_count), jnp.float32),
        pltpu.VMEM((2, BLK, max(w.shape[1] for w in weights)), jnp.float32),
    ]
    scratch += [pltpu.VMEM((2, 2 * w.shape[0], w.shape[1] // 2), jnp.bfloat16) for w in weights]
    scratch += [pltpu.VMEM((2 * rhs_count, max(sizes) // 2), jnp.bfloat16)]
    scratch += [pltpu.VMEM((rhs_count, count), jnp.float32) for count in pivots]
    for count in blocks + [count + 2 for count in blocks] + blocks[1:]:
        scratch += stripe_buffers(count)
    scratch += [
        pltpu.SemaphoreType.DMA((2,)),
        pltpu.SemaphoreType.DMA((copies,)),
        pltpu.SemaphoreType.DMA((copies,)),
    ]
    scratch += [pltpu.SemaphoreType.DMA((peers - 1,)) for _ in range(4)]
    vmem = pl.BlockSpec(memory_space=pltpu.VMEM)
    smem = pl.BlockSpec(memory_space=pltpu.SMEM)
    out = pl.pallas_call(
        functools.partial(solve_kernel, leaf_bits, front_bits, stripe_rows, pivots, sizes, cap),
        out_shape=jax.ShapeDtypeStruct((rows // 8, 8, rhs_count), jnp.float32),
        in_specs=[vmem] + [smem] * 4 + [pl.BlockSpec(memory_space=pl.ANY)] * 7,
        out_specs=vmem,
        scratch_shapes=scratch,
        compiler_params=pltpu.CompilerParams(
            collective_id=0, has_side_effects=True, vmem_limit_bytes=66 * 1024 * 1000
        ),
    )(app_rhs.reshape(rows, 1, rhs_count), *tables, *weights)
    return out.reshape(rows, rhs_count)


def slots_of(owner, order, row_count, cap):
    block = owner // row_count
    before = (block[:, None] == block[None, :]) & (order[None, :] < order[:, None])
    return block * cap + jnp.sum(before.astype(jnp.int32), axis=1)


def rows_of(slots, slot_count):
    rows = jnp.arange(slots.shape[0], dtype=jnp.int32)
    same = jnp.arange(slot_count, dtype=jnp.int32)[:, None] == slots[None, :]
    return jnp.sum(jnp.where(same, rows[None, :], 0), axis=1)


def per_device(app_rhs, pivot_source, row_owner, *matrices):
    row_count = app_rhs.shape[0]
    peer_count = lax.axis_size("leaf") * lax.axis_size("front")
    mean_rows = row_count // (peer_count // 2)
    cap = mean_rows + max(1, mean_rows // 4)
    send_slots = slots_of(row_owner, jnp.arange(row_count, dtype=jnp.int32), row_count, cap)
    recv_slots = slots_of(pivot_source, pivot_source, row_count, cap)
    tables = (
        rows_of(send_slots, peer_count * cap),
        recv_slots,
        rows_of(recv_slots, peer_count * cap),
        send_slots,
    )
    return solve(app_rhs, tables, [w[0, 0] for w in matrices], cap)


def solution(mesh):
    rows = P(("leaf", "front"), None)
    flat = P(("leaf", "front"))
    blocks = P("leaf", "front", None, None)
    return jax.shard_map(
        per_device, mesh=mesh, in_specs=(rows, flat, flat) + (blocks,) * 7, out_specs=rows, check_vma=False
    )
```

time: 263 us -> 216 us (0.82)
  waiting for transfers between devices: 51 us -> 0 us
  Pallas kernels: 179 us -> 207 us
  local copies, waits for them, and re-layouts: 17.5 us -> 1.78 us
  starting transfers between devices: 11.1 us -> 0 us
  other arithmetic: 3.87 us -> 6.51 us
    all_to_all x2 -> x0, waiting for transfers between devices: 51 us -> none  [move_rows(): lax.all_to_all(shaped, ('leaf', 'front'), split_axis=0, concat_axis=0, ti...]
    pallas_call x1, Pallas kernels: 179 us -> 207 us  [solve(): pl.pallas_call(functools.partial(solve_kernel, leaf_bits, front_bits, str...]
    all_to_all x2 -> x0, starting transfers between devices: 11.1 us -> none  [move_rows(): lax.all_to_all(shaped, ('leaf', 'front'), split_axis=0, concat_axis=0, ti...]
    scatter x2 -> x0, local copies, waits for them, and re-layouts: 9.83 us -> none  [the longest x1 5.03 us: per_device(): jnp.zeros((peer_count * slot_cap, rhs_count), jnp.float32).at[recv_index]]
    gather x2 -> x0, local copies, waits for them, and re-layouts: 4.57 us -> none  [the longest x1 2.29 us: per_device(): ordered = move_rows(outgoing, slot_cap)[recv_index]]
    reduce_sum x2 -> x3, other arithmetic: 0.65 us -> 3.71 us  [the longest x1 2.06 us: rows_of(): return jnp.sum(jnp.where(same, rows[None, :], 0), axis=1)]
  transfers between devices with their start and end apart: 2 -> 0, of which waited for: 2 -> 0; matrix products, arithmetic and copies ran while one was open for 0% -> 0% of each run, Pallas kernels for 0% -> 0%
where the time goes in v1:
time: 216 us; the launch traced here: 215 us
  Pallas kernels  207 us (96%)
  other arithmetic  6.51 us (3%)
    pallas_call x1, Pallas kernels, solve(): pl.pallas_call(functools.partial(solve_kernel, leaf_bits, front_bits, str...  207 us

profile of v1, /device:TPU:0, one launch (start us, length us, event | category | flops | bytes accessed | tf_op | source)
XLA Modules:
  0.0 215.4 jit_solution(10755033102779224644)
XLA Ops:
  0.0 0.7 add_select_fusion.1
  0.7 0.4 convert_reduce_fusion.1
  1.1 0.7 multiply_add_fusion.1.refs_4_
  1.8 0.0 copy-start
  1.8 0.7 add_select_fusion
  2.5 1.3 convert_reduce_fusion
  3.8 0.7 multiply_add_fusion.refs_2_
  4.5 0.0 copy-done
  4.5 0.0 copy-start.1
  4.5 2.1 select_reduce_fusion
  6.5 0.0 copy-done.1
  6.5 207.1 %shard_map.100 = f32[96,8,128]{2,1,0:T(8,128)} custom-call(f32[768,1,128]{2,1,0:T(1,128)} %bitcast.17, s32[1920]{0:T(1024)} %get-tuple-element.6.refs_1_, s32[768]{0:T(1024)} %copy-done.1, s32[1920]{0:T(1024)} %get-tuple-element.5.refs_3_, s32[768]{0:T(1024)} %copy-done, f32[384,1536]{1,0:T(8,128)} %bitcast.9, f32[384,1024]{1,0:T(8,128)} %bitcast.13, ...), custom_call_target="tpu_custom_call" | custom-call | tf_op jit(solution)/shard_map/pallas_call | solution.py:466
  213.6 1.8 copy.12
Async XLA Ops:
  1.8 2.7 %copy-start = (s32[768]{0:T(1024)}, s32[768]{0:T(1024)S(1)}, u32[]{:S(2)}) copy-start(s32[768]{0:T(1024)S(1)} %multiply_add_fusion.1.refs_4_) | copy-start | bytes 9220
  4.5 2.1 copy-start.1

commit v2 on v1

v2 whole, which is shorter than its diff:
```python
import functools

import jax
import jax.numpy as jnp
from jax import lax
from jax.experimental import pallas as pl
from jax.experimental.pallas import tpu as pltpu
from jax.sharding import PartitionSpec as P

BLK = 128
HEIGHTS = 4
CLASSES = 3
MESH = pl.DeviceIdType.MESH
CORE = ("front", 0)
GROUPS = 2
STRIPE_UNITS = (2, 2, 1, 1, 1, 1)


def bit_of(value, place):
    return lax.rem(lax.div(value, jnp.int32(2**place)), jnp.int32(2))


def flipped(value, mask, bits):
    out = jnp.int32(0)
    for place in range(bits):
        out = out + lax.rem(bit_of(value, place) + bit_of(mask, place), jnp.int32(2)) * 2**place
    return out


def group_dims(front_bits, height):
    return [("front", place) for place in range(1, front_bits)] + [("leaf", place) for place in range(height)]


def group_orders(front_bits, height):
    dims = group_dims(front_bits, height)
    turns = min(CLASSES, len(dims))
    head, rest = dims[:turns], dims[turns:]
    return [head[turn:] + head[:turn] + rest for turn in range(turns)]


def place_slot(place, height, order):
    slot = 0
    for axis, at in order:
        slot = slot * 2 + (place >> (at + height if axis == "front" else at) & 1)
    return slot


def place_lane(place):
    return bin(place).count("1") % 2


def split(value):
    high = value.astype(jnp.bfloat16)
    return high, (value - high.astype(jnp.float32)).astype(jnp.bfloat16)


def dot(left, right, right_axis):
    dims = (((1,), (right_axis,)), ((), ()))
    return lax.dot_general(left, right, dimension_numbers=dims, preferred_element_type=jnp.float32)


def solve_kernel(leaf_bits, front_bits, stripe_rows, pivots, sizes, cap, *refs):
    app_ref, pack_idx, order_idx, back_pack_idx, back_idx = refs[:5]
    weights_hbm = refs[5:12]
    out_ref = refs[12]
    packed, arrived, returned, ordered, sol, right_ref, done_ref = refs[13:20]
    near, far = refs[20:22]
    stacked = refs[22:29]
    left_ref = refs[29]
    solved = refs[30:34]
    pair_out, pair_in = refs[34:36]
    buffers = refs[36:-12]
    near_sems, far_send, far_recv, free_sem, pair_send, pair_recv = refs[-12:-6]
    send_sems, recv_sems, go_send, go_recv, back_send, back_recv = refs[-6:]
    stripes = len(stripe_rows)
    per_group = stripes // GROUPS
    width = sum(stripe_rows[:per_group])
    lows = [sum(stripe_rows[:s]) % width for s in range(stripes)]
    pos = 0

    def take(count):
        nonlocal pos
        pos += count
        return buffers[pos - count : pos]

    partial = [take(stripes) for _ in range(HEIGHTS)]
    recv = [take(stripes) for _ in range(HEIGHTS)]
    whole_vec = [partial[0]] + [take(stripes) for _ in range(HEIGHTS - 1)]

    leaf = lax.axis_index("leaf")
    front = lax.axis_index("front")
    fronts = 2**front_bits
    peers = 2 ** (front_bits + leaf_bits)
    here = {"leaf": leaf, "front": front}
    me = leaf * fronts + front

    def mine(dim):
        return bit_of(here[dim[0]], dim[1])

    core_flip = front + (1 - 2 * mine(CORE))

    def partner(dim):
        axis, place = dim
        if dim == CORE:
            return (leaf, core_flip)
        move = (1 - 2 * mine(dim)) * 2**place
        return (leaf + move, core_flip) if axis == "leaf" else (leaf, core_flip + move)

    def peer(step):
        turn = jnp.int32(peers - 1) - step
        return (
            flipped(leaf, lax.div(turn, jnp.int32(fronts)), leaf_bits),
            flipped(front, lax.rem(turn, jnp.int32(fronts)), front_bits),
        )

    piece_of = [pivots[h] // BLK for h in range(HEIGHTS)]
    halves = [size // BLK // 2 for size in sizes]
    orders = [group_orders(front_bits, h) for h in range(HEIGHTS)]
    lanes = []
    for height in range(HEIGHTS):
        total = jnp.int32(0)
        for place in range(front_bits):
            total = total + bit_of(front, place)
        for place in range(height):
            total = total + bit_of(leaf, place)
        lanes.append(lax.rem(total, jnp.int32(2)))

    def kind(height, stripe):
        return stripe % per_group % len(orders[height])

    places = []
    for height in range(HEIGHTS):
        table = {}
        for place in range(2 ** (front_bits + height)):
            if not place >> height & 1:
                table[place_slot(place, height, orders[height][0])] = place
        places.append(table)

    perms = []
    for height in range(HEIGHTS):
        table = [[0] * halves[height] for _ in orders[height]]
        for place in range(2 ** (front_bits + height)):
            canon = place_slot(place, height, orders[height][0])
            for k, order in enumerate(orders[height]):
                for part in range(piece_of[height]):
                    table[k][canon * piece_of[height] + part] = (
                        place_slot(place, height, order) * piece_of[height] + part
                    )
        perms.append(table)

    weight_heights = (0, 1, 1, 2, 2, 3, 3)
    pieces = []
    for index in range(7):
        for part in range(weights_hbm[index].shape[0] // BLK):
            pieces.append((index, part))

    def column(height, at, lane):
        piece = piece_of[height]
        place, rest = places[height][at // piece], at % piece
        core = lax.rem(lane + place_lane(place), jnp.int32(2))
        return pl.multiple_of((place * piece + rest) * BLK + core * (2**height * piece * BLK), BLK)

    def block_copies(number, lane):
        index, part = pieces[number]
        height = weight_heights[index]
        for at in range(halves[height]):
            yield at, weights_hbm[index].at[pl.ds(part * BLK, BLK), pl.ds(column(height, at, lane), BLK)]

    def start_near(number):
        for at, source in block_copies(number, lanes[weight_heights[pieces[number][0]]]):
            pltpu.make_async_copy(source, near.at[number % 2, at], near_sems.at[number % 2]).start()

    def far_copy(number, at, source):
        return pltpu.make_async_remote_copy(
            src_ref=source,
            dst_ref=at,
            send_sem=far_send.at[number % 2],
            recv_sem=far_recv.at[number % 2],
            device_id=(leaf, core_flip),
            device_id_type=MESH,
        )

    def start_far(number):
        for at, source in block_copies(number, 1 - lanes[weight_heights[pieces[number][0]]]):
            far_copy(number, far.at[number % 2, at], source).start()

    start_near(0)
    start_near(1)

    barrier = pltpu.get_barrier_semaphore()

    def greet(step, carry):
        pl.semaphore_signal(barrier, inc=1, device_id=peer(step), device_id_type=MESH)
        return carry

    lax.fori_loop(0, peers - 1, greet, 0)

    def pack_rows(index, source, target, base, where):
        for row in range(cap):
            target[base + row] = source(index[where + row])

    def send_to(step, source, target, sends, recvs):
        to_leaf, to_front = peer(step)
        there = to_leaf * fronts + to_front
        return pltpu.make_async_remote_copy(
            src_ref=source.at[pl.ds(there * cap, cap)],
            dst_ref=target.at[pl.ds(me * cap, cap)],
            send_sem=sends.at[0],
            recv_sem=recvs.at[0],
            device_id=(to_leaf, to_front),
            device_id_type=MESH,
        )

    def exchange_rows(index, source, target, sends, recvs, ready):
        def pack(step):
            to_leaf, to_front = peer(step)
            base = (to_leaf * fronts + to_front) * cap
            pack_rows(index, source, packed, base, base)

        if ready is not None:
            lax.fori_loop(0, peers - 1, lambda step, carry: (pack(step), carry)[1], 0)
            pack_rows(index, source, target, me * cap, me * cap)
            ready()

            def launch(step, carry):
                send_to(step, packed, target, sends, recvs).start()
                return carry

            lax.fori_loop(0, peers - 1, launch, 0)
            return

        pack(jnp.int32(0))

        def body(step, carry):
            pack(step)
            send_to(step - 1, packed, target, sends, recvs).start()
            return carry

        lax.fori_loop(1, peers - 1, body, 0)
        pack_rows(index, source, target, me * cap, me * cap)
        send_to(jnp.int32(peers - 2), packed, target, sends, recvs).start()

    def finish_rows(target, sends, recvs):
        for ref, sem in ((packed, sends), (target, recvs)):
            span = ref.at[pl.ds(0, (peers - 1) * cap)]
            pltpu.make_async_copy(span, span, sem.at[0]).wait()

    def unpack_rows(index, source, target):
        def body(group, carry):
            for row in range(8):
                target[group, pl.ds(row, 1), :] = source[index[group * 8 + row]]
            return carry

        lax.fori_loop(0, target.shape[0], body, 0, unroll=2)

    exchange_rows(
        pack_idx,
        lambda i: app_ref[i],
        arrived,
        go_send,
        go_recv,
        lambda: pl.semaphore_wait(barrier, peers - 1),
    )
    start_far(0)
    start_far(1)

    for number, (index, part) in enumerate(pieces):
        rows = weights_hbm[index].shape[0]
        half = halves[weight_heights[index]]
        slot = number % 2
        here_all, there_all = near.at[slot, pl.ds(0, half)], far.at[slot, pl.ds(0, half)]
        pltpu.make_async_copy(here_all, here_all, near_sems.at[slot]).wait()
        far_copy(number, there_all, there_all).wait()

        def convert(group, carry, index=index, part=part, rows=rows, half=half, slot=slot):
            span = pl.ds(pl.multiple_of(group * 16, 16), 16)
            for side, source in enumerate((near, far)):
                for at in range(half):
                    for level, value in enumerate(split(source[slot, at, span, :])):
                        start = (2 * side + level) * rows + part * BLK + group * 16
                        stacked[index][pl.ds(pl.multiple_of(start, 16), 16), pl.ds(at * BLK, BLK)] = value
            return carry

        lax.fori_loop(0, BLK // 16, convert, 0)
        if number + 2 < len(pieces):
            pl.semaphore_signal(free_sem, inc=1, device_id=(leaf, core_flip), device_id_type=MESH)
            start_near(number + 2)
            pl.semaphore_wait(free_sem, 1)
            start_far(number + 2)

    finish_rows(arrived, go_send, go_recv)
    unpack_rows(order_idx, arrived, ordered)

    all_dims = [CORE] + group_dims(front_bits, leaf_bits)

    def remote(source, target, dim, stripe, role):
        if role < 2:
            role = role * len(all_dims) + all_dims.index(dim)
        else:
            role = role - 2 + 2 * len(all_dims)
        index = role * stripes + stripe
        copy = pltpu.make_async_remote_copy(
            src_ref=source,
            dst_ref=target,
            send_sem=send_sems.at[stripe],
            recv_sem=recv_sems.at[index],
            device_id=partner(dim),
            device_id_type=MESH,
        )
        copy.start()
        return copy

    def members(group):
        return range(group * per_group, (group + 1) * per_group)

    def own_slot(height, stripe):
        slot = jnp.int32(0)
        for dim in orders[height][kind(height, stripe)]:
            slot = slot * 2 + mine(dim)
        return slot * piece_of[height]

    def reduce_steps(group, height, swap_at, bases):
        bufs, recvs, result = partial[height], recv[height], whole_vec[height]
        depth = len(orders[height][0])
        whole, prior, offset = halves[height], 0, 0
        pending = {}
        for step in range(depth + 1):
            full = swap_at is not None and step == depth - 1
            size = whole if full else whole // 2
            if full:
                offset = swap_at
            if step > 0:
                yield
            for s in members(group):
                if step > 0:
                    pending[s].wait()
                    keep = pl.ds(bases[s], whole)
                    (result if step == depth else bufs)[s][keep] = bufs[s][keep] + recvs[s][pl.ds(prior, whole)]
                if step < depth:
                    dim = orders[height][kind(height, s)][step]
                    away, role = bases[s], 0
                    if full:
                        role = 2 * height + (swap_at == halves[height])
                    else:
                        away = bases[s] + (1 - mine(dim)) * size
                        bases[s] = bases[s] + mine(dim) * size
                    pending[s] = remote(
                        bufs[s].at[pl.ds(away, size)], recvs[s].at[pl.ds(offset, size)], dim, s, role
                    )
            prior, whole = offset, size
            offset += size

    def gather_steps(group, height, bases, size, depth):
        bufs = whole_vec[height]
        pending = {}
        for step in range(depth - 1, -1, -1):
            for s in members(group):
                if pending.get(s) is not None:
                    pending[s].wait()
                dim = orders[height][kind(height, s)][step]
                span = pl.ds(bases[s], size)
                pending[s] = remote(bufs[s].at[span], bufs[s].at[span], dim, s, 1)
                bases[s] = bases[s] - mine(dim) * size
            size *= 2
            yield
        for s in members(group):
            pending[s].wait()

    turns = [0] * GROUPS

    def apply_rows(group, index, height, finish):
        bufs, half = whole_vec[height], halves[height]
        for at in range(half):
            block = jnp.concatenate(
                [bufs[s][perms[height][kind(height, s)][at]] for s in members(group)], axis=0
            )
            high, low = split(block)
            left_ref[0:width, at * BLK : (at + 1) * BLK] = high
            left_ref[width : 2 * width, at * BLK : (at + 1) * BLK] = low
        full = dot(left_ref[:, 0 : half * BLK], stacked[index][...], 1)
        both = full[:width] + full[width:]
        rows = both.shape[1] // 4
        turn = turns[group] % 2
        turns[group] += 1
        for side in range(2):
            low = 2 * side * rows
            pair_out[group, side, :, 0:rows] = both[:, low : low + rows] + both[:, low + rows : low + 2 * rows]
        copy = pltpu.make_async_remote_copy(
            src_ref=pair_out.at[group, :, :, pl.ds(0, rows)],
            dst_ref=pair_in.at[group, turn, :, :, pl.ds(0, rows)],
            send_sem=pair_send.at[group],
            recv_sem=pair_recv.at[2 * group + turn],
            device_id=(leaf, core_flip),
            device_id_type=MESH,
        )
        copy.start()
        yield
        copy.wait()
        finish(
            jnp.concatenate(
                [pair_out[group, side, :, 0:rows] + pair_in[group, turn, 1 - side, :, 0:rows] for side in range(2)],
                axis=1,
            )
        )

    def apply_cols(group, index, height, vector):
        bufs, half = partial[height], halves[height]
        rows = vector.shape[1] // 2
        sides = []
        for part in split(vector):
            near_part, far_part = part[:, :rows], part[:, rows:]
            sides.append(jnp.concatenate([near_part, near_part, far_part, far_part], axis=1))
        left = jnp.concatenate(sides, axis=0)
        for at in range(0, half, 2):
            full = dot(left, stacked[index][:, at * BLK : (at + 2) * BLK], 0)
            both = full[:width] + full[width:]
            for step in range(2):
                for s in members(group):
                    bufs[s][perms[height][kind(height, s)][at + step]] = both[
                        lows[s] : lows[s] + stripe_rows[s], step * BLK : (step + 1) * BLK
                    ]

    inverses = (0, 2, 4, 6)
    couplings = (1, 3, 5)
    starts = [sum(pivots[:h]) // BLK for h in range(HEIGHTS)]
    for part in range(right_ref.shape[0]):
        low = part * BLK // 8
        right_ref[part] = ordered[low : low + BLK // 8].reshape(BLK, -1).T

    def chain(group):
        def keep_value(height):
            def keep(value):
                solved[height][group] = value

            return keep

        def own_right(height, part, s):
            low = group * width + lows[s]
            return right_ref[starts[height] + part, low : low + stripe_rows[s]]

        bases = {s: own_slot(0, s) for s in members(group)}
        for part in range(piece_of[0]):
            for s in members(group):
                partial[0][s][bases[s] + part] = own_right(0, part, s)
        yield from gather_steps(group, 0, bases, piece_of[0], len(orders[0][0]))
        yield from apply_rows(group, inverses[0], 0, keep_value(0))
        for height in range(1, HEIGHTS):
            apply_cols(group, couplings[height - 1], height, -solved[height - 1][group])
            for s in members(group):
                spot, slot = partial[height][s], own_slot(height, s)
                spot[slot] = spot[slot] + own_right(height, 0, s)
            bases = {s: jnp.int32(0) for s in members(group)}
            yield from reduce_steps(group, height, halves[height] - 2, bases)
            yield from gather_steps(group, height, bases, 2, len(orders[height][0]) - 1)
            yield from apply_rows(group, inverses[height], height, keep_value(height))
        target = [solved[HEIGHTS - 1][group]]
        for height in range(HEIGHTS - 1, -1, -1):
            apply_cols(group, inverses[height], height, target.pop())
            bases = {s: jnp.int32(0) for s in members(group)}
            yield from reduce_steps(group, height, halves[height] if height > 0 else None, bases)
            for part in range(piece_of[height]):
                for s in members(group):
                    low = group * width + lows[s]
                    done_ref[starts[height] + part, low : low + stripe_rows[s]] = whole_vec[height][s][
                        own_slot(height, s) + part
                    ]
            if height > 0:
                yield from gather_steps(group, height, bases, 2, len(orders[height][0]) - 1)
                yield from apply_rows(
                    group,
                    couplings[height - 1],
                    height,
                    lambda value: target.append(solved[height - 1][group] - value),
                )

    chains = [chain(group) for group in range(GROUPS)]
    while chains:
        for running in list(chains):
            if next(running, chains) is chains:
                chains.remove(running)
    for part in range(done_ref.shape[0]):
        sol[part * BLK : (part + 1) * BLK, :] = done_ref[part].T

    exchange_rows(
        back_pack_idx, lambda i: sol[pl.ds(i, 1), :], returned, back_send, back_recv, None
    )
    finish_rows(returned, back_send, back_recv)
    unpack_rows(back_idx, returned, out_ref)


def solve(app_rhs, tables, weights, cap):
    leaves = lax.axis_size("leaf")
    fronts = lax.axis_size("front")
    peers = leaves * fronts
    front_bits = fronts.bit_length() - 1
    leaf_bits = leaves.bit_length() - 1
    rows, rhs_count = app_rhs.shape
    units = [unit * rhs_count // BLK for unit in STRIPE_UNITS * GROUPS]
    width = rhs_count // GROUPS
    stripe_rows = tuple(8 * unit for unit in units)
    inverses = (weights[0], weights[2], weights[4], weights[6])
    sizes = tuple(w.shape[1] for w in inverses)
    pivots = tuple(w.shape[0] for w in inverses)
    blocks = [size // BLK for size in sizes]

    def stripe_buffers(count):
        return [pltpu.VMEM((count, height, BLK), jnp.float32) for height in stripe_rows]

    copies = (2 * (1 + len(group_dims(front_bits, leaf_bits))) + 2 * (HEIGHTS - 1)) * len(stripe_rows)
    scratch = [
        pltpu.VMEM((peers * cap, 1, rhs_count), jnp.float32),
        pltpu.VMEM((peers * cap, 1, rhs_count), jnp.float32),
        pltpu.VMEM((peers * cap, 1, rhs_count), jnp.float32),
        pltpu.VMEM((rows // 8, 8, rhs_count), jnp.float32),
        pltpu.VMEM((rows, rhs_count), jnp.float32),
        pltpu.VMEM((rows // BLK, rhs_count, BLK), jnp.float32),
        pltpu.VMEM((rows // BLK, rhs_count, BLK), jnp.float32),
        pltpu.VMEM((2, max(blocks) // 2, BLK, BLK), jnp.float32),
        pltpu.VMEM((2, max(blocks) // 2, BLK, BLK), jnp.float32),
    ]
    scratch += [pltpu.VMEM((4 * w.shape[0], w.shape[1] // 2), jnp.bfloat16) for w in weights]
    scratch += [pltpu.VMEM((2 * width, max(sizes) // 2), jnp.bfloat16)]
    scratch += [pltpu.VMEM((GROUPS, width, 2 * count), jnp.float32) for count in pivots]
    scratch += [
        pltpu.VMEM((GROUPS, 2, width, max(pivots)), jnp.float32),
        pltpu.VMEM((GROUPS, 2, 2, width, max(pivots)), jnp.float32),
    ]
    lane_blocks = [count // 2 for count in blocks]
    for count in lane_blocks + [count + 2 for count in lane_blocks] + lane_blocks[1:]:
        scratch += stripe_buffers(count)
    scratch += [pltpu.SemaphoreType.DMA((2,)) for _ in range(3)]
    scratch += [pltpu.SemaphoreType.REGULAR]
    scratch += [pltpu.SemaphoreType.DMA((count,)) for count in (GROUPS, 2 * GROUPS)]
    scratch += [pltpu.SemaphoreType.DMA((count,)) for count in (len(stripe_rows), copies)]
    scratch += [pltpu.SemaphoreType.DMA((1,)) for _ in range(4)]
    vmem = pl.BlockSpec(memory_space=pltpu.VMEM)
    smem = pl.BlockSpec(memory_space=pltpu.SMEM)
    out = pl.pallas_call(
        functools.partial(solve_kernel, leaf_bits, front_bits, stripe_rows, pivots, sizes, cap),
        out_shape=jax.ShapeDtypeStruct((rows // 8, 8, rhs_count), jnp.float32),
        in_specs=[vmem] + [smem] * 4 + [pl.BlockSpec(memory_space=pl.ANY)] * 7,
        out_specs=vmem,
        scratch_shapes=scratch,
        compiler_params=pltpu.CompilerParams(
            collective_id=0, has_side_effects=True, vmem_limit_bytes=66 * 1024 * 1000
        ),
    )(app_rhs.reshape(rows, 1, rhs_count), *tables, *weights)
    return out.reshape(rows, rhs_count)


def slots_of(owner, order, row_count, cap):
    block = owner // row_count
    before = (block[:, None] == block[None, :]) & (order[None, :] < order[:, None])
    return block * cap + jnp.sum(before.astype(jnp.int32), axis=1)


def rows_of(slots, slot_count):
    rows = jnp.arange(slots.shape[0], dtype=jnp.int32)
    same = jnp.arange(slot_count, dtype=jnp.int32)[:, None] == slots[None, :]
    return jnp.sum(jnp.where(same, rows[None, :], 0), axis=1)


def per_device(app_rhs, pivot_source, row_owner, *matrices):
    row_count = app_rhs.shape[0]
    peer_count = lax.axis_size("leaf") * lax.axis_size("front")
    mean_rows = row_count // (peer_count // 2)
    cap = mean_rows + max(1, mean_rows // 4)
    send_slots = slots_of(row_owner, jnp.arange(row_count, dtype=jnp.int32), row_count, cap)
    recv_slots = slots_of(pivot_source, pivot_source, row_count, cap)
    tables = (
        rows_of(send_slots, peer_count * cap),
        recv_slots,
        rows_of(recv_slots, peer_count * cap),
        send_slots,
    )
    return solve(app_rhs, tables, [w[0, 0] for w in matrices], cap)


def solution(mesh):
    rows = P(("leaf", "front"), None)
    flat = P(("leaf", "front"))
    blocks = P("leaf", "front", None, None)
    return jax.shard_map(
        per_device, mesh=mesh, in_specs=(rows, flat, flat) + (blocks,) * 7, out_specs=rows, check_vma=False
    )
```

time: 216 us -> 191 us (0.88)
  Pallas kernels: 207 us -> 182 us
    pallas_call x1, Pallas kernels: 207 us -> 182 us  [solve(): pl.pallas_call(functools.partial(solve_kernel, leaf_bits, front_bits, str...]
where the time goes in v2:
time: 191 us; the launch traced here: 190 us
  Pallas kernels  182 us (95%)
  other arithmetic  6.51 us (3%)
    pallas_call x1, Pallas kernels, solve(): pl.pallas_call(functools.partial(solve_kernel, leaf_bits, front_bits, str...  182 us

profile of v2, /device:TPU:0, one launch (start us, length us, event | category | flops | bytes accessed | tf_op | source)
XLA Modules:
  0.0 190.5 jit_solution(4107285169320542361)
XLA Ops:
  0.0 0.7 add_select_fusion.1
  0.7 0.4 convert_reduce_fusion.1
  1.1 0.7 multiply_add_fusion.1.refs_4_
  1.8 0.0 copy-start
  1.8 0.7 add_select_fusion
  2.5 1.3 convert_reduce_fusion
  3.8 0.7 multiply_add_fusion.refs_2_
  4.5 0.0 copy-done
  4.5 0.0 copy-start.1
  4.5 2.1 %select_reduce_fusion = (s32[1920]{0:T(1024)}, s32[1920]{0:T(1024)}) fusion(s32[768]{0:T(1024)S(1)} %multiply_add_fusion.refs_2_, s32[768]{0:T(1024)S(1)} %multiply_add_fusion.1.refs_4_), kind=kLoop, calls=%fused_computation | loop fusion | flops 8843520 | bytes 21504 | tf_op jit(solution)/shard_map/reduce_sum | solution.py:560
  6.5 0.0 copy-done.1
  6.5 182.1 %shard_map.100 = f32[96,8,128]{2,1,0:T(8,128)} custom-call(f32[768,1,128]{2,1,0:T(1,128)} %bitcast.17, s32[1920]{0:T(1024)} %get-tuple-element.6.refs_1_, s32[768]{0:T(1024)} %copy-done.1, s32[1920]{0:T(1024)} %get-tuple-element.5.refs_3_, s32[768]{0:T(1024)} %copy-done, f32[384,1536]{1,0:T(8,128)} %bitcast.9, f32[384,1024]{1,0:T(8,128)} %bitcast.13, ...), custom_call_target="tpu_custom_call" | custom-call | tf_op jit(solution)/shard_map/pallas_call | solution.py:538
  188.7 1.8 copy.12
Async XLA Ops:
  1.8 2.7 %copy-start = (s32[768]{0:T(1024)}, s32[768]{0:T(1024)S(1)}, u32[]{:S(2)}) copy-start(s32[768]{0:T(1024)S(1)} %multiply_add_fusion.1.refs_4_) | copy-start | bytes 9220
  4.5 2.1 %copy-start.1 = (s32[768]{0:T(1024)}, s32[768]{0:T(1024)S(1)}, u32[]{:S(2)}) copy-start(s32[768]{0:T(1024)S(1)} %multiply_add_fusion.refs_2_) | copy-start | bytes 9220

commit v3 on v2

--- a/solution.py
+++ b/solution.py
@@ -36,6 +36,14 @@
     turns = min(CLASSES, len(dims))
     head, rest = dims[:turns], dims[turns:]
     return [head[turn:] + head[:turn] + rest for turn in range(turns)]
+
+
+def swap_steps(height):
+    return (0, 2, 2, 1)[height]
+
+
+def kept_blocks(front_bits, height, half):
+    return half >> (len(group_dims(front_bits, height)) - swap_steps(height))
 
 
 def place_slot(place, height, order):
@@ -189,11 +197,9 @@
 
     barrier = pltpu.get_barrier_semaphore()
 
-    def greet(step, carry):
+    def greet(step):
         pl.semaphore_signal(barrier, inc=1, device_id=peer(step), device_id_type=MESH)
-        return carry
-
-    lax.fori_loop(0, peers - 1, greet, 0)
+
 
     def pack_rows(index, source, target, base, where):
         for row in range(cap):
@@ -218,7 +224,13 @@
             pack_rows(index, source, packed, base, base)
 
         if ready is not None:
-            lax.fori_loop(0, peers - 1, lambda step, carry: (pack(step), carry)[1], 0)
+
+            def meet(step, carry):
+                greet(step)
+                pack(step)
+                return carry
+
+            lax.fori_loop(0, peers - 1, meet, 0)
             pack_rows(index, source, target, me * cap, me * cap)
             ready()
 
@@ -291,7 +303,7 @@
     finish_rows(arrived, go_send, go_recv)
     unpack_rows(order_idx, arrived, ordered)
 
-    all_dims = [CORE] + group_dims(front_bits, leaf_bits)
+    all_dims = group_dims(front_bits, leaf_bits)
 
     def remote(source, target, dim, stripe, role):
         if role < 2:
@@ -319,16 +331,19 @@
             slot = slot * 2 + mine(dim)
         return slot * piece_of[height]
 
-    def reduce_steps(group, height, swap_at, bases):
+    def reduce_steps(group, height, way, bases):
         bufs, recvs, result = partial[height], recv[height], whole_vec[height]
         depth = len(orders[height][0])
         whole, prior, offset = halves[height], 0, 0
+        swaps = swap_steps(height)
+        kept = kept_blocks(front_bits, height, whole)
         pending = {}
         for step in range(depth + 1):
-            full = swap_at is not None and step == depth - 1
+            full = depth - swaps <= step
             size = whole if full else whole // 2
+            number = way * swaps + step - depth + swaps
             if full:
-                offset = swap_at
+                offset = halves[height] - kept + number * kept
             if step > 0:
                 yield
             for s in members(group):
@@ -340,7 +355,7 @@
                     dim = orders[height][kind(height, s)][step]
                     away, role = bases[s], 0
                     if full:
-                        role = 2 * height + (swap_at == halves[height])
+                        role = 2 * height + (way if height == HEIGHTS - 1 else number % swaps)
                     else:
                         away = bases[s] + (1 - mine(dim)) * size
                         bases[s] = bases[s] + mine(dim) * size
@@ -363,8 +378,12 @@
                 bases[s] = bases[s] - mine(dim) * size
             size *= 2
             yield
-        for s in members(group):
-            pending[s].wait()
+        for copy in pending.values():
+            copy.wait()
+
+    def spread_steps(group, height, bases):
+        kept = kept_blocks(front_bits, height, halves[height])
+        return gather_steps(group, height, bases, kept, len(orders[height][0]) - swap_steps(height))
 
     turns = [0] * GROUPS
 
@@ -449,15 +468,15 @@
             for s in members(group):
                 spot, slot = partial[height][s], own_slot(height, s)
                 spot[slot] = spot[slot] + own_right(height, 0, s)
-            bases = {s: jnp.int32(0) for s in members(group)}
-            yield from reduce_steps(group, height, halves[height] - 2, bases)
-            yield from gather_steps(group, height, bases, 2, len(orders[height][0]) - 1)
+            bases = dict.fromkeys(members(group), 0)
+            yield from reduce_steps(group, height, 0, bases)
+            yield from spread_steps(group, height, bases)
             yield from apply_rows(group, inverses[height], height, keep_value(height))
         target = [solved[HEIGHTS - 1][group]]
         for height in range(HEIGHTS - 1, -1, -1):
             apply_cols(group, inverses[height], height, target.pop())
-            bases = {s: jnp.int32(0) for s in members(group)}
-            yield from reduce_steps(group, height, halves[height] if height > 0 else None, bases)
+            bases = dict.fromkeys(members(group), 0)
+            yield from reduce_steps(group, height, 1, bases)
             for part in range(piece_of[height]):
                 for s in members(group):
                     low = group * width + lows[s]
@@ -465,7 +484,7 @@
                         own_slot(height, s) + part
                     ]
             if height > 0:
-                yield from gather_steps(group, height, bases, 2, len(orders[height][0]) - 1)
+                yield from spread_steps(group, height, bases)
                 yield from apply_rows(
                     group,
                     couplings[height - 1],
@@ -506,7 +525,7 @@
     def stripe_buffers(count):
         return [pltpu.VMEM((count, height, BLK), jnp.float32) for height in stripe_rows]
 
-    copies = (2 * (1 + len(group_dims(front_bits, leaf_bits))) + 2 * (HEIGHTS - 1)) * len(stripe_rows)
+    roles = 2 * len(group_dims(front_bits, leaf_bits)) + 2 * (HEIGHTS - 1)
     scratch = [
         pltpu.VMEM((peers * cap, 1, rhs_count), jnp.float32),
         pltpu.VMEM((peers * cap, 1, rhs_count), jnp.float32),
@@ -526,12 +545,16 @@
         pltpu.VMEM((GROUPS, 2, 2, width, max(pivots)), jnp.float32),
     ]
     lane_blocks = [count // 2 for count in blocks]
-    for count in lane_blocks + [count + 2 for count in lane_blocks] + lane_blocks[1:]:
+    landing = []
+    for height, count in enumerate(lane_blocks):
+        kept = kept_blocks(front_bits, height, count)
+        landing.append(count - kept + 2 * swap_steps(height) * kept)
+    for count in lane_blocks + landing + lane_blocks[1:]:
         scratch += stripe_buffers(count)
     scratch += [pltpu.SemaphoreType.DMA((2,)) for _ in range(3)]
     scratch += [pltpu.SemaphoreType.REGULAR]
     scratch += [pltpu.SemaphoreType.DMA((count,)) for count in (GROUPS, 2 * GROUPS)]
-    scratch += [pltpu.SemaphoreType.DMA((count,)) for count in (len(stripe_rows), copies)]
+    scratch += [pltpu.SemaphoreType.DMA((count,)) for count in (len(stripe_rows), roles * len(stripe_rows))]
     scratch += [pltpu.SemaphoreType.DMA((1,)) for _ in range(4)]
     vmem = pl.BlockSpec(memory_space=pltpu.VMEM)
     smem = pl.BlockSpec(memory_space=pltpu.SMEM)

time: 191 us -> 182 us (0.953)
  Pallas kernels: 182 us -> 173 us
    pallas_call x1, Pallas kernels: 182 us -> 173 us  [solve(): pl.pallas_call(functools.partial(solve_kernel, leaf_bits, front_bits, str...]
where the time goes in v3:
time: 182 us
  Pallas kernels  173 us (95%)
  other arithmetic  6.51 us (4%)
    pallas_call x1, Pallas kernels, solve(): pl.pallas_call(functools.partial(solve_kernel, leaf_bits, front_bits, str...  173 us

profile of v3, /device:TPU:0, one launch (start us, length us, event | category | flops | bytes accessed | tf_op | source)
XLA Modules:
  0.0 181.5 jit_solution(7487194232459791042)
XLA Ops:
  0.0 0.7 add_select_fusion.1
  0.7 0.4 convert_reduce_fusion.1
  1.1 0.7 multiply_add_fusion.1.refs_4_
  1.8 0.0 copy-start
  1.8 0.7 add_select_fusion
  2.5 1.3 convert_reduce_fusion
  3.8 0.7 multiply_add_fusion.refs_2_
  4.5 0.0 copy-done
  4.5 0.0 copy-start.1
  4.5 2.1 %select_reduce_fusion = (s32[1920]{0:T(1024)}, s32[1920]{0:T(1024)}) fusion(s32[768]{0:T(1024)S(1)} %multiply_add_fusion.refs_2_, s32[768]{0:T(1024)S(1)} %multiply_add_fusion.1.refs_4_), kind=kLoop, calls=%fused_computation | loop fusion | flops 8843520 | bytes 21504 | tf_op jit(solution)/shard_map/reduce_sum | solution.py:583
  6.5 0.0 copy-done.1
  6.5 173.2 %shard_map.100 = f32[96,8,128]{2,1,0:T(8,128)} custom-call(f32[768,1,128]{2,1,0:T(1,128)} %bitcast.17, s32[1920]{0:T(1024)} %get-tuple-element.6.refs_1_, s32[768]{0:T(1024)} %copy-done.1, s32[1920]{0:T(1024)} %get-tuple-element.5.refs_3_, s32[768]{0:T(1024)} %copy-done, f32[384,1536]{1,0:T(8,128)} %bitcast.9, f32[384,1024]{1,0:T(8,128)} %bitcast.13, ...), custom_call_target="tpu_custom_call" | custom-call | tf_op jit(solution)/shard_map/pallas_call | solution.py:561
  179.7 1.8 copy.12
Async XLA Ops:
  1.8 2.7 %copy-start = (s32[768]{0:T(1024)}, s32[768]{0:T(1024)S(1)}, u32[]{:S(2)}) copy-start(s32[768]{0:T(1024)S(1)} %multiply_add_fusion.1.refs_4_) | copy-start | bytes 9220
  4.5 2.1 %copy-start.1 = (s32[768]{0:T(1024)}, s32[768]{0:T(1024)S(1)}, u32[]{:S(2)}) copy-start(s32[768]{0:T(1024)S(1)} %multiply_add_fusion.refs_2_) | copy-start | bytes 9220

commit v4 on v3

--- a/solution.py
+++ b/solution.py
@@ -13,7 +13,7 @@
 MESH = pl.DeviceIdType.MESH
 CORE = ("front", 0)
 GROUPS = 2
-STRIPE_UNITS = (2, 2, 1, 1, 1, 1)
+STRIPE_UNITS = (1,) * 8
 
 
 def bit_of(value, place):
@@ -571,16 +571,19 @@
     return out.reshape(rows, rhs_count)
 
 
-def slots_of(owner, order, row_count, cap):
-    block = owner // row_count
-    before = (block[:, None] == block[None, :]) & (order[None, :] < order[:, None])
-    return block * cap + jnp.sum(before.astype(jnp.int32), axis=1)
+def slots_of(owners, row_count, cap):
+    owners = lax.optimization_barrier(owners)
+    block = lax.optimization_barrier(owners // row_count)
+    sent = lax.broadcasted_iota(jnp.int32, owners.shape, 0) == 0
+    order = jnp.where(sent, lax.broadcasted_iota(jnp.int32, owners.shape, 1), owners)
+    before = (block[:, :, None] == block[:, None, :]) & (order[:, None, :] < order[:, :, None])
+    return lax.optimization_barrier(block * cap + jnp.sum(before.astype(jnp.int32), axis=2))
 
 
 def rows_of(slots, slot_count):
-    rows = jnp.arange(slots.shape[0], dtype=jnp.int32)
-    same = jnp.arange(slot_count, dtype=jnp.int32)[:, None] == slots[None, :]
-    return jnp.sum(jnp.where(same, rows[None, :], 0), axis=1)
+    rows = jnp.arange(slots.shape[1], dtype=jnp.int32)
+    same = jnp.arange(slot_count, dtype=jnp.int32)[None, :, None] == slots[:, None, :]
+    return jnp.sum(jnp.where(same, rows[None, None, :], 0), axis=2)
 
 
 def per_device(app_rhs, pivot_source, row_owner, *matrices):
@@ -588,14 +591,9 @@
     peer_count = lax.axis_size("leaf") * lax.axis_size("front")
     mean_rows = row_count // (peer_count // 2)
     cap = mean_rows + max(1, mean_rows // 4)
-    send_slots = slots_of(row_owner, jnp.arange(row_count, dtype=jnp.int32), row_count, cap)
-    recv_slots = slots_of(pivot_source, pivot_source, row_count, cap)
-    tables = (
-        rows_of(send_slots, peer_count * cap),
-        recv_slots,
-        rows_of(recv_slots, peer_count * cap),
-        send_slots,
-    )
+    slots = slots_of(jnp.stack([row_owner, pivot_source]), row_count, cap)
+    rows = rows_of(slots, peer_count * cap)
+    tables = (rows[0], slots[1], rows[1], slots[0])
     return solve(app_rhs, tables, [w[0, 0] for w in matrices], cap)
 
 

time: 182 us -> 180 us (0.989)
  other arithmetic: 6.51 us -> 2.65 us
  local copies, waits for them, and re-layouts: 1.78 us -> 4.4 us
    reduce_sum x3 -> x2, other arithmetic: 3.71 us -> 2.55 us  [the longest x1 1.47 us: rows_of(): return jnp.sum(jnp.where(same, rows[None, None, :], 0), axis=2)]
where the time goes in v4:
time: 180 us; the launch traced here: 179 us
  Pallas kernels  172 us (96%)
  local copies, waits for them, and re-layouts  4.4 us (2%)
  other arithmetic  2.65 us (1%)
    pallas_call x1, Pallas kernels, solve(): pl.pallas_call(functools.partial(solve_kernel, leaf_bits, front_bits, str...  172 us

profile of v4, /device:TPU:0, one launch (start us, length us, event | category | flops | bytes accessed | tf_op | source)
XLA Modules:
  0.0 179.4 jit_solution(10898988287712215304)
XLA Ops:
  0.0 0.7 stack.10
  0.7 0.7 stack.9
  1.4 0.1 and_select_fusion
  1.5 1.1 convert_reduce_fusion
  2.6 0.6 slice_reduce_fusion.2
  3.2 1.5 select_reduce_fusion
  4.7 0.6 slice_reduce_fusion
  5.3 172.4 %shard_map.100 = f32[96,8,128]{2,1,0:T(8,128)} custom-call(f32[768,1,128]{2,1,0:T(1,128)} %bitcast.17, s32[1920]{0:T(1024)} %get-tuple-element.6.refs_1_, s32[768]{0:T(1024)} %get-tuple-element.8.refs_2_, s32[1920]{0:T(1024)} %get-tuple-element.5.refs_3_, s32[768]{0:T(1024)} %get-tuple-element.7.refs_4_, f32[384,1536]{1,0:T(8,128)} %bitcast.9, ...), custom_call_target="tpu_custom_call" | custom-call | tf_op jit(solution)/shard_map/pallas_call | solution.py:561
  177.7 1.8 copy.12
  (3 shorter events, 0.0 us)
